TPU v7x, 256 devices: a whole 4x4x8 slice. The times are simulated.
256 devices in a mesh: expert: 8 (over x, core), replica: 32 (over y, z).
Axes of the slice: x: 4, y: 4, z: 8, core: 2. Of those that a mesh axis runs over, the one named last changes fastest.
Arguments:
- tokens: bfloat16 [1536, 4096], P(('expert', 'replica')), may hold values from -6 to 6
- out_grad: bfloat16 [1536, 4096], P(('expert', 'replica')), may hold values from -2.5 to 2.5
- expert_ids: int32 [1536, 2], P(('expert', 'replica')), may hold values from 0 to 7, all different within a row; in each aligned block of 6 rows (0 to 5, 6 to 11, ...) at most 2 rows name the same one
- gates: float32 [1536, 2], P(('expert', 'replica')), may hold values from 0.1 to 1
- w_gate: bfloat16 [8, 7168, 4096], P('expert', 'replica'), may hold values from -0.09375 to 0.09375
- w_up: bfloat16 [8, 7168, 4096], P('expert', 'replica'), may hold values from -0.09375 to 0.09375
- w_down: bfloat16 [8, 7168, 4096], P('expert', 'replica'), may hold values from -0.0625 to 0.0625
Outputs:
- gate_grad: float32 [1536, 2], P(('expert', 'replica'))
- input_grad: bfloat16 [1536, 4096], P(('expert', 'replica'))
- grad_gate: bfloat16 [8, 7168, 4096], P('expert', 'replica')
- grad_up: bfloat16 [8, 7168, 4096], P('expert', 'replica')
- grad_down: bfloat16 [8, 7168, 4096], P('expert', 'replica')
Inputs may be any that keep to these rules, and one draw needn't show every extreme that they name: `expert_ids`: each row names 2 different experts; among the rows of one device no expert is named more than 2 times.
All inputs are finite; a program needn't handle non-finite values.
Results may differ from a plain program's by a relative error of at most 0.02.
Values may be sent and summed in bfloat16 or wider, within the bound.
No kernel may reach another device: no remote copies, remote signals or barrier semaphores. Data moves between devices by JAX's collectives and lax.ppermute only.
A program may use at most 128 MiB of HBM per device.

v0:
```python
import jax
import jax.numpy as jnp
from jax import lax
from jax.sharding import Mesh
from jax.sharding import PartitionSpec as P

REPLICA = ("replica_0", "replica_1")
EXPERT_REPLICA = ("expert", "replica_0", "replica_1")


def split_up(value, dim, peers):
    shape = value.shape
    tiles = value.reshape(*shape[:dim], peers, shape[dim] // peers, *shape[dim + 1 :])
    return jnp.moveaxis(tiles, dim, 0)


def sum_at_owner(value, axis, dim):
    peers = lax.axis_size(axis)
    tiles = lax.all_to_all(split_up(value, dim, peers), axis, 0, 0, tiled=True)
    return jnp.sum(tiles, axis=0)


def own_rows(terms, axes):
    running = terms.astype(jnp.bfloat16)
    for axis in axes:
        running = lax.psum_scatter(running, axis, scatter_dimension=0, tiled=True)
    return running.astype(jnp.float32)


def on_device(tokens, out_grad, expert_ids, gates, w_gate, w_up, w_down):
    token_count = tokens.shape[0]
    fan_out = expert_ids.shape[1]
    model_width = tokens.shape[1]
    owners = lax.axis_size("expert")
    capacity = max(2, 4 * token_count * fan_out // (3 * owners))
    slot_count = owners * capacity
    flat_ids = expert_ids.reshape(-1)
    sequence_pos = jnp.arange(token_count * fan_out, dtype=jnp.int32)
    earlier = sequence_pos[None, :] < sequence_pos[:, None]
    same_expert = flat_ids[:, None] == flat_ids[None, :]
    slot_rank = jnp.sum(jnp.logical_and(same_expert, earlier), axis=1)
    target = flat_ids * capacity + slot_rank
    token_hot = (target[:, None] == jnp.arange(slot_count, dtype=jnp.int32)[None, :]).astype(
        jnp.float32
    )
    token_hot = token_hot.reshape(token_count, fan_out, slot_count)
    dispatch = jnp.sum(token_hot, axis=1).astype(jnp.bfloat16)
    slot_gate = jnp.sum(token_hot * gates[:, :, None], axis=(0, 1)).reshape(owners, capacity)
    leading = (((0,), (0,)), ((), ()))
    contract = (((1,), (1,)), ((), ()))
    send_inputs = (
        lax.dot_general(dispatch, tokens, leading, preferred_element_type=jnp.float32)
        .astype(jnp.bfloat16)
        .reshape(owners, capacity, model_width)
    )
    send_grads = (
        lax.dot_general(dispatch, out_grad, leading, preferred_element_type=jnp.float32)
        .astype(jnp.bfloat16)
        .reshape(owners, capacity, model_width)
    )
    gate_weight = w_gate[0]
    up_weight = w_up[0]
    down_weight = w_down[0]
    owned = (
        lax.all_to_all(send_inputs, "expert", split_axis=0, concat_axis=0, tiled=True),
        lax.all_to_all(send_grads, "expert", split_axis=0, concat_axis=0, tiled=True),
        lax.all_to_all(
            slot_gate.astype(jnp.bfloat16), "expert", split_axis=0, concat_axis=0, tiled=True
        ).astype(slot_gate.dtype),
    )
    column_inputs, column_grads, column_gates = (
        lax.all_gather(owned[0], REPLICA, axis=0, tiled=True),
        lax.all_gather(owned[1], REPLICA, axis=0, tiled=True),
        lax.all_gather(owned[2].astype(jnp.bfloat16), REPLICA, axis=0, tiled=True).astype(
            jnp.float32
        ),
    )
    gathered = column_inputs.reshape(-1, model_width)
    gate_pre = lax.dot_general(gathered, gate_weight, contract, preferred_element_type=jnp.float32)
    up_pre = lax.dot_general(gathered, up_weight, contract, preferred_element_type=jnp.float32)
    sigmoid_gate = jax.nn.sigmoid(gate_pre)
    active = gate_pre * sigmoid_gate
    hidden = (active * up_pre).astype(jnp.bfloat16)
    gathered_grad = column_grads.reshape(-1, model_width)
    row_gates = column_gates.reshape(-1)
    full_out = jnp.dot(hidden, down_weight, preferred_element_type=jnp.float32)
    partial_value = jnp.sum(gathered_grad * full_out, axis=1)
    summed_products = sum_at_owner(partial_value, REPLICA, 0)
    returned = lax.all_to_all(
        summed_products.reshape(owners, capacity), "expert", split_axis=0, concat_axis=0, tiled=True
    )
    gate_grad = jnp.sum(token_hot * returned.reshape(-1)[None, None, :], axis=2)
    scaled = (row_gates[:, None] * gathered_grad).astype(jnp.bfloat16)
    hidden_grad = lax.dot_general(scaled, down_weight, contract, preferred_element_type=jnp.float32)
    gate_pre_grad = (
        hidden_grad * up_pre * sigmoid_gate * (1.0 + gate_pre * (1.0 - sigmoid_gate))
    ).astype(jnp.bfloat16)
    up_pre_grad = (hidden_grad * active).astype(jnp.bfloat16)
    grad_down = lax.dot_general(hidden, scaled, leading, preferred_element_type=jnp.float32).astype(
        jnp.bfloat16
    )
    grad_gate = lax.dot_general(
        gate_pre_grad, gathered, leading, preferred_element_type=jnp.float32
    ).astype(jnp.bfloat16)
    grad_up = lax.dot_general(
        up_pre_grad, gathered, leading, preferred_element_type=jnp.float32
    ).astype(jnp.bfloat16)
    slot_grad = own_rows(
        jnp.dot(gate_pre_grad, gate_weight, preferred_element_type=jnp.float32)
        + jnp.dot(up_pre_grad, up_weight, preferred_element_type=jnp.float32),
        REPLICA,
    ).astype(jnp.bfloat16)
    slot_back = lax.all_to_all(
        slot_grad.reshape(owners, capacity, model_width),
        "expert",
        split_axis=0,
        concat_axis=0,
        tiled=True,
    )
    slot_back = slot_back.reshape(slot_count, model_width)
    input_grad = jnp.dot(dispatch, slot_back, preferred_element_type=jnp.float32).astype(
        jnp.bfloat16
    )
    return (gate_grad, input_grad, grad_gate[None], grad_up[None], grad_down[None])


def solution(mesh):
    torus = Mesh(
        mesh.devices.reshape(mesh.shape["expert"], 4, 8), ("expert", "replica_0", "replica_1")
    )
    in_specs = (
        P(EXPERT_REPLICA, None),
        P(EXPERT_REPLICA, None),
        P(EXPERT_REPLICA, None),
        P(EXPERT_REPLICA, None),
        P("expert", REPLICA, None),
        P("expert", REPLICA, None),
        P("expert", REPLICA, None),
    )
    out_specs = (
        P(EXPERT_REPLICA, None),
        P(EXPERT_REPLICA, None),
        P("expert", REPLICA, None),
        P("expert", REPLICA, None),
        P("expert", REPLICA, None),
    )
    return jax.shard_map(
        on_device, mesh=torus, in_specs=in_specs, out_specs=out_specs, check_vma=False
    )
```

profile of v0, /device:TPU:1, one launch (start us, length us, event | category | flops | bytes accessed | tf_op | source)
XLA Modules:
  0.0 404.9 jit_solution(4118786558378128443)
XLA Ops:
  7.2 0.9 copy.30
  8.6 1.1 convolution_convert_fusion.3
  9.8 11.5 %all_to_all.42 = bf16[8,2,4096]{2,1,0:T(2,128)(2,1)} all-to-all(bf16[8,2,4096]{2,1,0:T(2,128)(2,1)S(1)} %reshape.81), channel_id=1, replica_groups=mesh['expert'=8,'replica_0'=4,'replica_1'=8] {'expert'}, dimensions={0} | all-to-all | bytes 262144 | tf_op jit(solution)/shard_map/all_to_all | solution.py:65
  21.3 1.1 convolution_convert_fusion.4
  22.5 9.2 %all_to_all.43 = bf16[8,2,4096]{2,1,0:T(2,128)(2,1)} all-to-all(bf16[8,2,4096]{2,1,0:T(2,128)(2,1)S(1)} %reshape.80), channel_id=1, replica_groups=mesh['expert'=8,'replica_0'=4,'replica_1'=8] {'expert'}, dimensions={0} | all-to-all | bytes 262144 | tf_op jit(solution)/shard_map/all_to_all | solution.py:66
  31.7 68.7 %all-gather.6.cloned.1.call-done = bf16[256,2,4096]{2,1,0:T(2,128)(2,1)} async-done(((bf16[8,2,4096]{2,1,0:T(2,128)(2,1)}), bf16[256,2,4096]{2,1,0:T(2,128)(2,1)}) %all-gather.6.cloned.1.call-update) | async-done | bytes 4194320 | tf_op jit(solution)/shard_map/all_gather | solution.py:72
  100.4 7.2 %reshape.82 = bf16[512,4096]{1,0:T(8,128)(2,1)} reshape(bf16[256,2,4096]{2,1,0:T(2,128)(2,1)} %all-gather.6.cloned.1.call-done) | data formatting | bytes 8388608 | tf_op jit(solution)/shard_map/reshape | solution.py:78
  107.6 4.3 %fusion.12 = f32[512,224]{0,1:T(8,128)S(1)} fusion(bf16[512,4096]{1,0:T(8,128)(2,1)} %reshape.82, bf16[1,224,4096]{2,1,0:T(8,128)(2,1)} %param.11), kind=kOutput, calls=%fused_computation.22 | convolution fusion | flops 939524096 | bytes 6488064 | tf_op jit(solution)/shard_map/dot_general | solution.py:79
  112.0 2.3 multiply_convert_fusion.5
  114.3 67.3 %all-gather.4.cloned.1.call-done = bf16[256,2,4096]{2,1,0:T(2,128)(2,1)} async-done(((bf16[8,2,4096]{2,1,0:T(2,128)(2,1)}), bf16[256,2,4096]{2,1,0:T(2,128)(2,1)}) %all-gather.4.cloned.1.call-update) | async-done | bytes 4194320 | tf_op jit(solution)/shard_map/all_gather | solution.py:73
  181.6 7.6 %reshape.85 = f32[512,4096]{1,0:T(8,128)} reshape(bf16[256,2,4096]{2,1,0:T(2,128)(2,1)} %all-gather.4.cloned.1.call-done) | data formatting | bytes 12582912 | tf_op jit(solution)/shard_map/convert_element_type | solution.py:87
  189.2 5.3 %multiply_reduce_fusion = f32[512]{0:T(512)S(1)} fusion(f32[512,4096]{1,0:T(8,128)} %reshape.85, bf16[512,224]{0,1:T(8,128)(2,1)S(1)} %get-tuple-element.14, bf16[1,224,4096]{2,1,0:T(8,128)(2,1)} %param.13), kind=kOutput, calls=%fused_computation.3 | convolution fusion | flops 943717888 | bytes 10455040 | tf_op jit(solution)/shard_map/dot_general | solution.py:86
  194.6 14.5 %all_to_all.44 = f32[32,1,16]{2,1,0:T(1,128)S(1)} all-to-all(f32[32,1,16]{2,1,0:T(1,128)S(1)} %bitcast.46), channel_id=1, replica_groups=mesh['expert'=8,'replica_0'=4,'replica_1'=8] {'replica_0','replica_1'}, dimensions={0} | all-to-all | bytes 4096 | tf_op jit(solution)/shard_map/all_to_all | solution.py:19
  209.1 0.7 all_to_all.31
  209.8 8.9 %all-to-all-start.3 = ((f32[8,1,2]{2,1,0:T(1,128)}), f32[8,1,2]{2,1,0:T(1,128)S(1)}, u32[]{:S(2)}, u32[]{:S(2)}) async-start(f32[8,1,2]{2,1,0:T(1,128)} %bitcast.4), calls=%async_computation.3 | async-start | bytes 8192 | tf_op jit(solution)/shard_map/all_to_all | solution.py:89
  218.8 4.4 %all-to-all-done.3 = f32[8,1,2]{2,1,0:T(1,128)S(1)} async-done(((f32[8,1,2]{2,1,0:T(1,128)}), f32[8,1,2]{2,1,0:T(1,128)S(1)}, u32[]{:S(2)}, u32[]{:S(2)}) %all-to-all-start.3) | async-done | bytes 96 | tf_op jit(solution)/shard_map/all_to_all | solution.py:89
  224.8 7.6 %all_to_all.45 = bf16[8,1,2]{2,1,0:T(2,128)(2,1)S(1)} all-to-all(bf16[8,1,2]{2,1,0:T(2,128)(2,1)S(1)} %convert_element_type.102), channel_id=1, replica_groups=mesh['expert'=8,'replica_0'=4,'replica_1'=8] {'expert'}, dimensions={0} | all-to-all | bytes 64 | tf_op jit(solution)/shard_map/all_to_all | solution.py:67
  232.4 31.3 %all-gather = bf16[256,1,2]{2,1,0:T(2,128)(2,1)S(1)} all-gather(bf16[8,1,2]{2,1,0:T(2,128)(2,1)S(1)} %all_to_all.45), channel_id=2, replica_groups=mesh['expert'=8,'replica_0'=4,'replica_1'=8] {'replica_0','replica_1'}, dimensions={0}, use_global_device_ids=true | all-gather | bytes 1056 | tf_op jit(solution)/shard_map/all_gather | solution.py:74
  263.8 10.4 %multiply_convert_fusion.1 = bf16[256,2,4096]{2,1,0:T(2,128)(2,1)} fusion(f32[256,2]{1,0:T(8,128)S(1)} %bitcast.45, bf16[256,2,4096]{2,1,0:T(2,128)(2,1)} %all-gather.4.cloned.1.call-done), kind=kLoop, calls=%fused_computation.2 | loop fusion | flops 6291456 | bytes 8390656 | tf_op jit(solution)/shard_map/convert_element_type | solution.py:93
  274.2 7.2 %convert_element_type.91 = bf16[512,4096]{1,0:T(8,128)(2,1)} reshape(bf16[256,2,4096]{2,1,0:T(2,128)(2,1)} %multiply_convert_fusion.1) | data formatting | bytes 8388608 | tf_op jit(solution)/shard_map/convert_element_type | solution.py:93
  281.4 4.4 %multiply_convert_fusion.3 = (bf16[512,224]{0,1:T(8,128)(2,1)S(1)}, bf16[512,224]{0,1:T(8,128)(2,1)S(1)}) fusion(f32[512,224]{0,1:T(8,128)S(1)} %fusion.12, f32[512,224]{0,1:T(8,128)} %get-tuple-element.15, bf16[512,4096]{1,0:T(8,128)(2,1)} %convert_element_type.91, bf16[1,224,4096]{2,1,0:T(8,128)(2,1)} %param.13), kind=kOutput, calls=%fused_computation.24 | convolution fusion | flops 941015040 | bytes 7405568 | tf_op jit(solution)/shard_map/dot_general | solution.py:94
  285.8 1.3 fusion.10
  287.1 3.3 add_convert_fusion
  290.7 53.7 %reduce-scatter.3.cloned.1.call-done = bf16[128,4096]{1,0:T(8,128)(2,1)} async-done(((bf16[512,4096]{1,0:T(8,128)(2,1)}), bf16[128,4096]{1,0:T(8,128)(2,1)}) %reduce-scatter.3.cloned.1.call-update) | async-done | bytes 1048592 | tf_op jit(solution)/shard_map/reduce_scatter | solution.py:26
  345.6 4.5 %fusion.1 = bf16[1,224,4096]{2,1,0:T(8,128)(2,1)} fusion(bf16[512,224]{0,1:T(8,128)(2,1)S(1)} %get-tuple-element.12, bf16[512,4096]{1,0:T(8,128)(2,1)} %reshape.82), kind=kOutput, calls=%fused_computation.8 | convolution fusion | flops 940441600 | bytes 6258688 | tf_op jit(solution)/shard_map/dot_general | solution.py:105
  350.2 5.8 %fusion.2 = bf16[1,224,4096]{2,1,0:T(8,128)(2,1)} fusion(bf16[512,224]{0,1:T(8,128)(2,1)S(1)} %get-tuple-element.14, f32[512,4096]{1,0:T(8,128)} %reshape.85, f32[512]{0:T(512)S(1)} %mul.80), kind=kOutput, calls=%fused_computation.9 | convolution fusion | flops 944635904 | bytes 10455040 | tf_op jit(solution)/shard_map/dot_general | solution.py:99
  356.0 24.6 %reduce-scatter.5.cloned.1.call-done = bf16[16,4096]{1,0:T(8,128)(2,1)} async-done(((bf16[128,4096]{1,0:T(8,128)(2,1)}), bf16[16,4096]{1,0:T(8,128)(2,1)}) %reduce-scatter.5.cloned.1.call-update) | async-done | bytes 131088 | tf_op jit(solution)/shard_map/reduce_scatter | solution.py:26
  380.6 1.6 reshape.83
  382.3 10.0 %all-to-all-start.5 = ((bf16[8,2,4096]{2,1,0:T(2,128)(2,1)}), bf16[8,2,4096]{2,1,0:T(2,128)(2,1)S(1)}, u32[]{:S(2)}, u32[]{:S(2)}) async-start(bf16[8,2,4096]{2,1,0:T(2,128)(2,1)} %reshape.83), calls=%async_computation.7 | async-start | bytes 262144 | tf_op jit(solution)/shard_map/all_to_all | solution.py:113
  392.3 4.5 %fusion = bf16[1,224,4096]{2,1,0:T(8,128)(2,1)} fusion(bf16[512,224]{0,1:T(8,128)(2,1)S(1)} %get-tuple-element.13, bf16[512,4096]{1,0:T(8,128)(2,1)} %reshape.82), kind=kOutput, calls=%fused_computation.7 | convolution fusion | flops 940441600 | bytes 6258688 | tf_op jit(solution)/shard_map/dot_general | solution.py:102
  396.8 0.7 all-to-all-done.5
  397.6 0.8 convolution_convert_fusion.5
  (36 shorter events, 4.1 us)
Async XLA Ops:
  7.2 104.8 %copy-start = (bf16[1,224,4096]{2,1,0:T(8,128)(2,1)S(1)}, bf16[1,224,4096]{2,1,0:T(8,128)(2,1)}, u32[]{:S(2)}) copy-start(bf16[1,224,4096]{2,1,0:T(8,128)(2,1)} %param.12) | copy-start | bytes 5505028
  7.2 93.2 %all-gather.6.cloned.1.call-start = ((), (), s32[]{:S(2)}) async-start(), calls=%async_computation.9 | async-start | bytes 4325376 | tf_op jit(solution)/shard_map/all_gather | solution.py:72
  21.3 160.3 %all-gather.4.cloned.1.call-start = ((), (), s32[]{:S(2)}) async-start(), calls=%async_computation.8 | async-start | bytes 4325376 | tf_op jit(solution)/shard_map/all_gather | solution.py:73
  107.6 4.4 %copy-start.1 = (bf16[512,4096]{1,0:T(8,128)(2,1)S(1)}, bf16[512,4096]{1,0:T(8,128)(2,1)}, u32[]{:S(2)}) copy-start(bf16[512,4096]{1,0:T(8,128)(2,1)} %reshape.82) | copy-start | bytes 12582916
  189.2 29.6 %copy-start.3 = (f32[6,2]{0,1:T(2,128)S(1)}, f32[6,2]{0,1:T(2,128)}, u32[]{:S(2)}) copy-start(f32[6,2]{0,1:T(2,128)} %param.10) | copy-start | bytes 148
  209.8 13.5 %all-to-all-start.3 = ((f32[8,1,2]{2,1,0:T(1,128)}), f32[8,1,2]{2,1,0:T(1,128)S(1)}, u32[]{:S(2)}, u32[]{:S(2)}) async-start(f32[8,1,2]{2,1,0:T(1,128)} %bitcast.4), calls=%async_computation.3 | async-start | bytes 8192 | tf_op jit(solution)/shard_map/all_to_all | solution.py:89
  218.7 125.7 %reduce-scatter.3.cloned.1.call-start = ((), (), s32[]{:S(2)}) async-start(), calls=%async_computation.10 | async-start | bytes 5242880 | tf_op jit(solution)/shard_map/reduce_scatter | solution.py:26
  281.4 4.4 %copy-start.2 = (bf16[1,224,4096]{2,1,0:T(8,128)(2,1)S(1)}, bf16[1,224,4096]{2,1,0:T(8,128)(2,1)}, u32[]{:S(2)}) copy-start(bf16[1,224,4096]{2,1,0:T(8,128)(2,1)} %param.11) | copy-start | bytes 5505028
  290.5 90.2 %reduce-scatter.5.cloned.1.call-start = ((), (), s32[]{:S(2)}) async-start(), calls=%async_computation.11 | async-start | bytes 1179648 | tf_op jit(solution)/shard_map/reduce_scatter | solution.py:26
  382.3 15.3 %all-to-all-start.5 = ((bf16[8,2,4096]{2,1,0:T(2,128)(2,1)}), bf16[8,2,4096]{2,1,0:T(2,128)(2,1)S(1)}, u32[]{:S(2)}, u32[]{:S(2)}) async-start(bf16[8,2,4096]{2,1,0:T(2,128)(2,1)} %reshape.83), calls=%async_computation.7 | async-start | bytes 262144 | tf_op jit(solution)/shard_map/all_to_all | solution.py:113
Sparse Core Ops, SparseCore 0:
  21.4 78.9 all-gather.5
  103.0 78.5 all-gather.3
  290.6 53.7 reduce-scatter.2
  346.8 33.7 reduce-scatter.4
where the time goes:
time: 406 us; the launch traced here: 405 us
  waiting for transfers between devices  220 us (54%)
  blocking collectives  74 us (18%)
  matrix products  38.8 us (10%)
  local copies, waits for them, and re-layouts  27.3 us (7%)
  starting transfers between devices  19.3 us (5%)
  between operations  13.9 us (3%)
  other arithmetic  12.1 us (3%)
    reduce_scatter x2, waiting for transfers between devices, own_rows(): running = lax.psum_scatter(running, axis, scatter_dimension=0, tiled=True)  78.3 us
    all_gather x1, waiting for transfers between devices, on_device(): lax.all_gather(owned[0], REPLICA, axis=0, tiled=True)  68.7 us
    all_gather x1, waiting for transfers between devices, on_device(): lax.all_gather(owned[1], REPLICA, axis=0, tiled=True)  67.3 us
    all_gather x1, blocking collectives, on_device(): lax.all_gather(owned[2].astype(jnp.bfloat16), REPLICA, axis=0, tiled=True)  31.3 us
    all_to_all x1, blocking collectives, sum_at_owner(): tiles = lax.all_to_all(split_up(value, dim, peers), axis, 0, 0, tiled=True)  14.5 us
    all_to_all x1, blocking collectives, on_device(): lax.all_to_all(send_inputs, 'expert', split_axis=0, concat_axis=0, tiled=...  11.5 us
    convert_element_type x1, other arithmetic, on_device(): scaled = (row_gates[:, None] * gathered_grad).astype(jnp.bfloat16)  10.4 us
    all_to_all x1, starting transfers between devices, on_device(): lax.all_to_all(slot_grad.reshape(owners, capacity, model_width), 'expert'...  10 us
  transfers between devices with their start and end apart: 6, of which 6 were waited for; matrix products, arithmetic and copies ran while one was open for 8% of the time, Pallas kernels for 0%

commit v1 on v0

--- a/solution.py
+++ b/solution.py
@@ -69,7 +69,15 @@
         ).astype(slot_gate.dtype),
     )
     column_inputs, column_grads, column_gates = (
-        lax.all_gather(owned[0], REPLICA, axis=0, tiled=True),
+        jnp.concatenate(
+            lax.all_to_all(
+                jnp.stack([owned[0]] * lax.axis_size(REPLICA)),
+                axis_name=REPLICA,
+                split_axis=0,
+                concat_axis=0,
+            ),
+            axis=0,
+        ),
         lax.all_gather(owned[1], REPLICA, axis=0, tiled=True),
         lax.all_gather(owned[2].astype(jnp.bfloat16), REPLICA, axis=0, tiled=True).astype(
             jnp.float32

time: 406 us -> 397 us (0.978)
  waiting for transfers between devices: 220 us -> 194 us
  starting transfers between devices: 19.3 us -> 32.3 us
  local copies, waits for them, and re-layouts: 27.3 us -> 34.2 us
    all_to_all x0 -> x2, waiting for transfers between devices: none -> 108 us  [the longest x1 104 us: on_device(): lax.all_to_all(jnp.stack([owned[0]] * lax.axis_size(REPLICA)), axis_name=...]
    all_gather x1 -> x0, waiting for transfers between devices: 68.7 us -> none  [on_device(): lax.all_gather(owned[0], REPLICA, axis=0, tiled=True)]
    all_gather x1, waiting for transfers between devices: 67.3 us -> 0.75 us  [on_device(): lax.all_gather(owned[1], REPLICA, axis=0, tiled=True)]
    all_to_all x0 -> x2, starting transfers between devices: none -> 17.1 us  [the longest x1 10.6 us: on_device(): lax.all_to_all(jnp.stack([owned[0]] * lax.axis_size(REPLICA)), axis_name=...]
    another operation x0 -> x2, local copies, waits for them, and re-layouts: none -> 13.4 us  [the longest x1 7.22 us: on_device(): gathered = column_inputs.reshape(-1, model_width)]
    all_to_all x1 -> x0, blocking collectives: 11.5 us -> none  [on_device(): lax.all_to_all(send_inputs, 'expert', split_axis=0, concat_axis=0, tiled=...]
    all_to_all x1, blocking collectives: 14.5 us -> 23.1 us  [sum_at_owner(): tiles = lax.all_to_all(split_up(value, dim, peers), axis, 0, 0, tiled=True)]
    reshape x1 -> x0, local copies, waits for them, and re-layouts: 7.22 us -> none  [on_device(): gathered = column_inputs.reshape(-1, model_width)]
  transfers between devices with their start and end apart: 6 -> 7, of which waited for: 6 -> 7; matrix products, arithmetic and copies ran while one was open for 8% -> 8% of each run, Pallas kernels for 0% -> 0%
where the time goes in v1:
time: 397 us; the launch traced here: 396 us
  waiting for transfers between devices  194 us (49%)
  blocking collectives  71.1 us (18%)
  matrix products  38.9 us (10%)
  local copies, waits for them, and re-layouts  34.2 us (9%)
  starting transfers between devices  32.3 us (8%)
  between operations  13.9 us (4%)
  other arithmetic  12.1 us (3%)
    all_to_all x1, waiting for transfers between devices, on_device(): lax.all_to_all(jnp.stack([owned[0]] * lax.axis_size(REPLICA)), axis_name=...  104 us
    reduce_scatter x2, waiting for transfers between devices, own_rows(): running = lax.psum_scatter(running, axis, scatter_dimension=0, tiled=True)  79 us
    all_gather x1, blocking collectives, on_device(): lax.all_gather(owned[2].astype(jnp.bfloat16), REPLICA, axis=0, tiled=True)  31.3 us
    all_to_all x1, blocking collectives, sum_at_owner(): tiles = lax.all_to_all(split_up(value, dim, peers), axis, 0, 0, tiled=True)  23.1 us
    all_to_all x1, starting transfers between devices, on_device(): lax.all_to_all(jnp.stack([owned[0]] * lax.axis_size(REPLICA)), axis_name=...  10.6 us
    convert_element_type x1, other arithmetic, on_device(): scaled = (row_gates[:, None] * gathered_grad).astype(jnp.bfloat16)  10.4 us
    all_to_all x1, starting transfers between devices, on_device(): lax.all_to_all(slot_grad.reshape(owners, capacity, model_width), 'expert'...  9.51 us
    all_to_all x1, blocking collectives, on_device(): lax.all_to_all(send_grads, 'expert', split_axis=0, concat_axis=0, tiled=T...  9.15 us
  transfers between devices with their start and end apart: 7, of which 7 were waited for; matrix products, arithmetic and copies ran while one was open for 8% of the time, Pallas kernels for 0%

profile of v1, /device:TPU:1, one launch (start us, length us, event | category | flops | bytes accessed | tf_op | source)
XLA Modules:
  0.0 396.1 jit_solution(1610069984219690643)
XLA Ops:
  7.2 0.9 copy.30
  8.5 1.1 convolution_convert_fusion.3
  10.4 6.5 %all-to-all-start.1 = ((bf16[8,2,4096]{2,1,0:T(2,128)(2,1)}), bf16[8,2,4096]{2,1,0:T(2,128)(2,1)S(1)}, u32[]{:S(2)}, u32[]{:S(2)}) async-start(bf16[8,2,4096]{2,1,0:T(2,128)(2,1)} %reshape.80), calls=%async_computation.1 | async-start | bytes 262144 | tf_op jit(solution)/shard_map/all_to_all | solution.py:65
  16.8 1.1 convolution_convert_fusion.4
  18.0 4.1 %all-to-all-done.1 = bf16[8,2,4096]{2,1,0:T(2,128)(2,1)S(1)} async-done(((bf16[8,2,4096]{2,1,0:T(2,128)(2,1)}), bf16[8,2,4096]{2,1,0:T(2,128)(2,1)S(1)}, u32[]{:S(2)}, u32[]{:S(2)}) %all-to-all-start.1) | async-done | bytes 131104 | tf_op jit(solution)/shard_map/all_to_all | solution.py:65
  22.1 9.2 %all_to_all.47 = bf16[8,2,4096]{2,1,0:T(2,128)(2,1)} all-to-all(bf16[8,2,4096]{2,1,0:T(2,128)(2,1)S(1)} %reshape.79), channel_id=1, replica_groups=mesh['expert'=8,'replica_0'=4,'replica_1'=8] {'expert'}, dimensions={0} | all-to-all | bytes 262144 | tf_op jit(solution)/shard_map/all_to_all | solution.py:66
  31.3 6.2 %stack.2 = bf16[32,8,2,4096]{3,2,1,0:T(2,128)(2,1)} broadcast(bf16[8,2,4096]{2,1,0:T(2,128)(2,1)S(1)} %all-to-all-done.1), dimensions={1,2,3} | broadcast | bytes 4325376 | tf_op jit(solution)/shard_map/stack | solution.py:74
  37.5 10.6 %all-to-all-start.2 = ((bf16[32,8,2,4096]{3,2,1,0:T(2,128)(2,1)}), bf16[32,8,2,4096]{3,2,1,0:T(2,128)(2,1)}, u32[]{:S(2)}, u32[]{:S(2)}) async-start(bf16[32,8,2,4096]{3,2,1,0:T(2,128)(2,1)} %stack.2), calls=%async_computation.2 | async-start | bytes 8388608 | tf_op jit(solution)/shard_map/all_to_all | solution.py:73
  48.8 104.0 %all-to-all-done.2 = bf16[32,8,2,4096]{3,2,1,0:T(2,128)(2,1)} async-done(((bf16[32,8,2,4096]{3,2,1,0:T(2,128)(2,1)}), bf16[32,8,2,4096]{3,2,1,0:T(2,128)(2,1)}, u32[]{:S(2)}, u32[]{:S(2)}) %all-to-all-start.2) | async-done | bytes 4194336 | tf_op jit(solution)/shard_map/all_to_all | solution.py:73
  152.9 7.2 %reshape_reshape.3 = bf16[512,4096]{1,0:T(8,128)(2,1)} reshape(bf16[32,8,2,4096]{3,2,1,0:T(2,128)(2,1)} %all-to-all-done.2) | data formatting | bytes 8388608 | tf_op jit(solution)/shard_map/reshape;reshape | solution.py:86
  160.1 4.4 %fusion.12 = f32[512,224]{0,1:T(8,128)S(1)} fusion(bf16[512,4096]{1,0:T(8,128)(2,1)} %reshape_reshape.3, bf16[1,224,4096]{2,1,0:T(8,128)(2,1)} %param.11), kind=kOutput, calls=%fused_computation.22 | convolution fusion | flops 939524096 | bytes 6488064 | tf_op jit(solution)/shard_map/dot_general | solution.py:87
  164.5 2.3 multiply_convert_fusion.5
  167.5 7.6 %reshape.83 = f32[512,4096]{1,0:T(8,128)} reshape(bf16[256,2,4096]{2,1,0:T(2,128)(2,1)} %all-gather.3.cloned.1.call-done) | data formatting | bytes 12582912 | tf_op jit(solution)/shard_map/convert_element_type | solution.py:95
  175.1 5.3 %multiply_reduce_fusion = f32[512]{0:T(512)S(1)} fusion(f32[512,4096]{1,0:T(8,128)} %reshape.83, bf16[512,224]{0,1:T(8,128)(2,1)S(1)} %get-tuple-element.14, bf16[1,224,4096]{2,1,0:T(8,128)(2,1)} %param.13), kind=kOutput, calls=%fused_computation.3 | convolution fusion | flops 943717888 | bytes 10455040 | tf_op jit(solution)/shard_map/dot_general | solution.py:94
  180.5 23.1 %all_to_all.48 = f32[32,1,16]{2,1,0:T(1,128)S(1)} all-to-all(f32[32,1,16]{2,1,0:T(1,128)S(1)} %bitcast.46), channel_id=1, replica_groups=mesh['expert'=8,'replica_0'=4,'replica_1'=8] {'replica_0','replica_1'}, dimensions={0} | all-to-all | bytes 4096 | tf_op jit(solution)/shard_map/all_to_all | solution.py:19
  204.4 5.4 %all-to-all-start.4 = ((f32[8,1,2]{2,1,0:T(1,128)}), f32[8,1,2]{2,1,0:T(1,128)S(1)}, u32[]{:S(2)}, u32[]{:S(2)}) async-start(f32[8,1,2]{2,1,0:T(1,128)} %bitcast.4), calls=%async_computation.4 | async-start | bytes 8192 | tf_op jit(solution)/shard_map/all_to_all | solution.py:97
  209.9 4.4 %all-to-all-done.4 = f32[8,1,2]{2,1,0:T(1,128)S(1)} async-done(((f32[8,1,2]{2,1,0:T(1,128)}), f32[8,1,2]{2,1,0:T(1,128)S(1)}, u32[]{:S(2)}, u32[]{:S(2)}) %all-to-all-start.4) | async-done | bytes 96 | tf_op jit(solution)/shard_map/all_to_all | solution.py:97
  215.8 7.6 %all_to_all.49 = bf16[8,1,2]{2,1,0:T(2,128)(2,1)S(1)} all-to-all(bf16[8,1,2]{2,1,0:T(2,128)(2,1)S(1)} %convert_element_type.102), channel_id=1, replica_groups=mesh['expert'=8,'replica_0'=4,'replica_1'=8] {'expert'}, dimensions={0} | all-to-all | bytes 64 | tf_op jit(solution)/shard_map/all_to_all | solution.py:67
  223.5 31.3 %all-gather = bf16[256,1,2]{2,1,0:T(2,128)(2,1)S(1)} all-gather(bf16[8,1,2]{2,1,0:T(2,128)(2,1)S(1)} %all_to_all.49), channel_id=2, replica_groups=mesh['expert'=8,'replica_0'=4,'replica_1'=8] {'replica_0','replica_1'}, dimensions={0}, use_global_device_ids=true | all-gather | bytes 1056 | tf_op jit(solution)/shard_map/all_gather | solution.py:82
  254.9 10.4 %multiply_convert_fusion.1 = bf16[256,2,4096]{2,1,0:T(2,128)(2,1)} fusion(f32[256,2]{1,0:T(8,128)S(1)} %bitcast.45, bf16[256,2,4096]{2,1,0:T(2,128)(2,1)} %all-gather.3.cloned.1.call-done), kind=kLoop, calls=%fused_computation.2 | loop fusion | flops 6291456 | bytes 8390656 | tf_op jit(solution)/shard_map/convert_element_type | solution.py:101
  265.2 7.2 %convert_element_type.91 = bf16[512,4096]{1,0:T(8,128)(2,1)} reshape(bf16[256,2,4096]{2,1,0:T(2,128)(2,1)} %multiply_convert_fusion.1) | data formatting | bytes 8388608 | tf_op jit(solution)/shard_map/convert_element_type | solution.py:101
  272.4 4.4 %multiply_convert_fusion.3 = (bf16[512,224]{0,1:T(8,128)(2,1)S(1)}, bf16[512,224]{0,1:T(8,128)(2,1)S(1)}) fusion(f32[512,224]{0,1:T(8,128)S(1)} %fusion.12, f32[512,224]{0,1:T(8,128)} %get-tuple-element.15, bf16[512,4096]{1,0:T(8,128)(2,1)} %convert_element_type.91, bf16[1,224,4096]{2,1,0:T(8,128)(2,1)} %param.13), kind=kOutput, calls=%fused_computation.24 | convolution fusion | flops 941015040 | bytes 7405568 | tf_op jit(solution)/shard_map/dot_general | solution.py:102
  276.9 1.3 fusion.10
  278.2 3.3 add_convert_fusion
  281.8 53.7 %reduce-scatter.3.cloned.1.call-done = bf16[128,4096]{1,0:T(8,128)(2,1)} async-done(((bf16[512,4096]{1,0:T(8,128)(2,1)}), bf16[128,4096]{1,0:T(8,128)(2,1)}) %reduce-scatter.3.cloned.1.call-update) | async-done | bytes 1048592 | tf_op jit(solution)/shard_map/reduce_scatter | solution.py:26
  336.7 4.5 %fusion.1 = bf16[1,224,4096]{2,1,0:T(8,128)(2,1)} fusion(bf16[512,224]{0,1:T(8,128)(2,1)S(1)} %get-tuple-element.12, bf16[512,4096]{1,0:T(8,128)(2,1)} %reshape_reshape.3), kind=kOutput, calls=%fused_computation.8 | convolution fusion | flops 940441600 | bytes 6258688 | tf_op jit(solution)/shard_map/dot_general | solution.py:113
  341.2 5.8 %fusion.2 = bf16[1,224,4096]{2,1,0:T(8,128)(2,1)} fusion(bf16[512,224]{0,1:T(8,128)(2,1)S(1)} %get-tuple-element.14, f32[512,4096]{1,0:T(8,128)} %reshape.83, f32[512]{0:T(512)S(1)} %mul.80), kind=kOutput, calls=%fused_computation.9 | convolution fusion | flops 944635904 | bytes 10455040 | tf_op jit(solution)/shard_map/dot_general | solution.py:107
  347.1 25.3 %reduce-scatter.5.cloned.1.call-done = bf16[16,4096]{1,0:T(8,128)(2,1)} async-done(((bf16[128,4096]{1,0:T(8,128)(2,1)}), bf16[16,4096]{1,0:T(8,128)(2,1)}) %reduce-scatter.5.cloned.1.call-update) | async-done | bytes 131088 | tf_op jit(solution)/shard_map/reduce_scatter | solution.py:26
  372.3 1.6 reshape.81
  374.0 9.5 %all-to-all-start.6 = ((bf16[8,2,4096]{2,1,0:T(2,128)(2,1)}), bf16[8,2,4096]{2,1,0:T(2,128)(2,1)S(1)}, u32[]{:S(2)}, u32[]{:S(2)}) async-start(bf16[8,2,4096]{2,1,0:T(2,128)(2,1)} %reshape.81), calls=%async_computation.8 | async-start | bytes 262144 | tf_op jit(solution)/shard_map/all_to_all | solution.py:121
  383.5 4.5 %fusion = bf16[1,224,4096]{2,1,0:T(8,128)(2,1)} fusion(bf16[512,224]{0,1:T(8,128)(2,1)S(1)} %get-tuple-element.13, bf16[512,4096]{1,0:T(8,128)(2,1)} %reshape_reshape.3), kind=kOutput, calls=%fused_computation.7 | convolution fusion | flops 940441600 | bytes 6258688 | tf_op jit(solution)/shard_map/dot_general | solution.py:110
  388.8 0.8 convolution_convert_fusion.5
  (37 shorter events, 7.5 us)
Async XLA Ops:
  7.2 157.3 %copy-start = (bf16[1,224,4096]{2,1,0:T(8,128)(2,1)S(1)}, bf16[1,224,4096]{2,1,0:T(8,128)(2,1)}, u32[]{:S(2)}) copy-start(bf16[1,224,4096]{2,1,0:T(8,128)(2,1)} %param.12) | copy-start | bytes 5505028
  10.4 11.7 %all-to-all-start.1 = ((bf16[8,2,4096]{2,1,0:T(2,128)(2,1)}), bf16[8,2,4096]{2,1,0:T(2,128)(2,1)S(1)}, u32[]{:S(2)}, u32[]{:S(2)}) async-start(bf16[8,2,4096]{2,1,0:T(2,128)(2,1)} %reshape.80), calls=%async_computation.1 | async-start | bytes 262144 | tf_op jit(solution)/shard_map/all_to_all | solution.py:65
  37.5 115.4 %all-to-all-start.2 = ((bf16[32,8,2,4096]{3,2,1,0:T(2,128)(2,1)}), bf16[32,8,2,4096]{3,2,1,0:T(2,128)(2,1)}, u32[]{:S(2)}, u32[]{:S(2)}) async-start(bf16[32,8,2,4096]{3,2,1,0:T(2,128)(2,1)} %stack.2), calls=%async_computation.2 | async-start | bytes 8388608 | tf_op jit(solution)/shard_map/all_to_all | solution.py:73
  48.1 119.4 %all-gather.3.cloned.1.call-start = ((), (), s32[]{:S(2)}) async-start(), calls=%async_computation.9 | async-start | bytes 4325376 | tf_op jit(solution)/shard_map/all_gather | solution.py:81
  160.1 4.4 %copy-start.1 = (bf16[512,4096]{1,0:T(8,128)(2,1)S(1)}, bf16[512,4096]{1,0:T(8,128)(2,1)}, u32[]{:S(2)}) copy-start(bf16[512,4096]{1,0:T(8,128)(2,1)} %reshape_reshape.3) | copy-start | bytes 12582916
  175.1 34.7 %copy-start.3 = (f32[6,2]{0,1:T(2,128)S(1)}, f32[6,2]{0,1:T(2,128)}, u32[]{:S(2)}) copy-start(f32[6,2]{0,1:T(2,128)} %param.10) | copy-start | bytes 148
  204.4 10.0 %all-to-all-start.4 = ((f32[8,1,2]{2,1,0:T(1,128)}), f32[8,1,2]{2,1,0:T(1,128)S(1)}, u32[]{:S(2)}, u32[]{:S(2)}) async-start(f32[8,1,2]{2,1,0:T(1,128)} %bitcast.4), calls=%async_computation.4 | async-start | bytes 8192 | tf_op jit(solution)/shard_map/all_to_all | solution.py:97
  209.8 125.7 %reduce-scatter.3.cloned.1.call-start = ((), (), s32[]{:S(2)}) async-start(), calls=%async_computation.10 | async-start | bytes 5242880 | tf_op jit(solution)/shard_map/reduce_scatter | solution.py:26
  272.4 4.4 %copy-start.2 = (bf16[1,224,4096]{2,1,0:T(8,128)(2,1)S(1)}, bf16[1,224,4096]{2,1,0:T(8,128)(2,1)}, u32[]{:S(2)}) copy-start(bf16[1,224,4096]{2,1,0:T(8,128)(2,1)} %param.11) | copy-start | bytes 5505028
  281.5 90.8 %reduce-scatter.5.cloned.1.call-start = ((), (), s32[]{:S(2)}) async-start(), calls=%async_computation.11 | async-start | bytes 1179648 | tf_op jit(solution)/shard_map/reduce_scatter | solution.py:26
  374.0 14.8 %all-to-all-start.6 = ((bf16[8,2,4096]{2,1,0:T(2,128)(2,1)}), bf16[8,2,4096]{2,1,0:T(2,128)(2,1)S(1)}, u32[]{:S(2)}, u32[]{:S(2)}) async-start(bf16[8,2,4096]{2,1,0:T(2,128)(2,1)} %reshape.81), calls=%async_computation.8 | async-start | bytes 262144 | tf_op jit(solution)/shard_map/all_to_all | solution.py:121
Sparse Core Ops, SparseCore 0:
  51.5 115.9 all-gather.2
  281.7 53.7 reduce-scatter.2
  338.0 34.2 reduce-scatter.4
